TPU v7x, 32 devices: a whole 2x2x4 slice. The times are simulated.
32 devices in a mesh: cache: 8 (over z, y), group: 4 (over x, core).
Axes of the slice: x: 2, y: 2, z: 4, core: 2. Of those that a mesh axis runs over, the one named last changes fastest.
Arguments:
- queries: bfloat16 [32, 4096], P('cache'), may hold values from -240 to 240
- request_of: int32 [32], P('cache'), may hold values from 0 to 1, as said below
- selected: int32 [32, 8, 4], P('cache', 'group'), may hold values from 0 to 15, as said below
- cache_keys: bfloat16 [2, 8, 2048, 128], P(None, 'group', 'cache'), may hold values from -6 to 6
- cache_values: bfloat16 [2, 8, 2048, 128], P(None, 'group', 'cache'), may hold values from -6 to 6
- recent_keys: bfloat16 [32, 8, 1024, 128], P('cache', None, 'group'), may hold values from -6 to 6
- recent_values: bfloat16 [32, 8, 1024, 128], P('cache', None, 'group'), may hold values from -6 to 6
Outputs:
- attended: bfloat16 [32, 4096], P('cache', 'group')
Inputs may be any that keep to these rules, and one draw needn't show every extreme that they name: `request_of`: each prompt is read by exactly 16 slots. `selected`: for each slot and key-value head the 4 block ids have distinct owners id // 2; the 4 slots of one index of cache, with the key-value heads of one index of group, select at most 4 blocks held by any one owner, and exactly 4 from some owner.
All inputs are finite; a program needn't handle non-finite values.
Results may differ from a plain program's by a relative error of at most 0.0015.
Values may be sent and summed in bfloat16 or wider, within the bound.
No kernel may reach another device: no remote copies, remote signals or barrier semaphores. Data moves between devices by JAX's collectives and lax.ppermute only.
A program may use at most 64 MiB of HBM per device.

v0:
```python
import jax
import jax.numpy as jnp
from jax import lax
from jax.sharding import PartitionSpec as P

BLOCK = 128


def partial_attention(query_heads, key_rows, value_rows, score_scale):
    scores = (
        jnp.einsum("rhgd,rhnd->rhgn", query_heads, key_rows, preferred_element_type=jnp.float32)
        * score_scale
    )
    highest = jnp.max(scores, axis=-1)
    exponent = jnp.exp(scores - highest[..., None])
    totals = jnp.sum(exponent, axis=-1)
    summed = jnp.einsum(
        "rhgn,rhnd->rhgd", exponent, value_rows.astype(jnp.float32), precision=lax.Precision.HIGHEST
    )
    return (summed, highest, totals)


def combine(summed, highest, totals):
    peak_value = jnp.max(highest, axis=0)
    factor = jnp.exp(highest - peak_value[None])
    weight = jnp.sum(factor * totals, axis=0)
    return jnp.sum(factor[..., None] * summed, axis=0) / weight[..., None]


def owner_plan(
    all_prompts,
    all_selected,
    cache_keys,
    cache_values,
    owner_count,
    row_count,
    mine_heads,
    top_count,
    head_dim,
):
    per_owner = cache_keys.shape[2] // BLOCK
    wanted = row_count * mine_heads * top_count
    capacity = (wanted + owner_count - 1) // owner_count
    entry = jnp.arange(wanted, dtype=jnp.int32)
    dest_selected = all_selected.reshape(owner_count, wanted)
    held_here = dest_selected // per_owner == lax.axis_index("cache")
    rank_here = jnp.cumsum(held_here.astype(jnp.int32), axis=1) - 1
    place = jnp.arange(capacity, dtype=jnp.int32)
    picks = held_here[:, None, :] & (rank_here[:, None, :] == place[None, :, None])
    slot_entry = jnp.sum(jnp.where(picks, entry[None, None, :], 0), axis=2)
    slot_block = jnp.sum(jnp.where(picks, dest_selected[:, None, :], 0), axis=2) % per_owner
    slot_row = slot_entry // (mine_heads * top_count)
    slot_head = slot_entry // top_count % mine_heads
    slot_prompt = jnp.take_along_axis(all_prompts.reshape(owner_count, row_count), slot_row, axis=1)
    key_blocks = cache_keys.reshape(cache_keys.shape[0], mine_heads, per_owner, BLOCK, head_dim)[
        slot_prompt, slot_head, slot_block
    ]
    value_blocks = cache_values.reshape(
        cache_values.shape[0], mine_heads, per_owner, BLOCK, head_dim
    )[slot_prompt, slot_head, slot_block]
    return (slot_row, slot_head, key_blocks, value_blocks)


def per_device(queries, request_of, selected, cache_keys, cache_values, recent_keys, recent_values):
    row_count = queries.shape[0]
    heads_kv = recent_keys.shape[1]
    head_dim = recent_keys.shape[3]
    per_kv = queries.shape[1] // (heads_kv * head_dim)
    mine_heads = selected.shape[1]
    top_count = selected.shape[2]
    score_scale = head_dim ** (-0.5)
    all_heads = queries.reshape(row_count, heads_kv, per_kv, head_dim)
    own_heads = lax.dynamic_slice_in_dim(
        all_heads, lax.axis_index("group") * mine_heads, mine_heads, 1
    )
    owner_count = lax.axis_size("cache")
    per_owner = cache_keys.shape[2] // BLOCK
    wanted = row_count * mine_heads * top_count
    entry = jnp.arange(wanted, dtype=jnp.int32)
    own_flat = selected.reshape(wanted)
    source = own_flat // per_owner
    earlier = (source[:, None] == source[None, :]) & (entry[None, :] < entry[:, None])
    source_rank = jnp.sum(earlier.astype(jnp.int32), axis=1)
    all_prompts, all_selected = (
        lax.all_gather(request_of, "cache", axis=0, tiled=True),
        lax.all_gather(selected, "cache", axis=0, tiled=True),
    )
    slot_row, slot_head, key_blocks, value_blocks = owner_plan(
        all_prompts,
        all_selected,
        cache_keys,
        cache_values,
        owner_count,
        row_count,
        mine_heads,
        top_count,
        head_dim,
    )
    got_keys, got_values = (
        lax.all_to_all(key_blocks, "cache", split_axis=0, concat_axis=0, tiled=True),
        lax.all_to_all(value_blocks, "cache", split_axis=0, concat_axis=0, tiled=True),
    )
    picked_keys = got_keys[source, source_rank].reshape(
        row_count, mine_heads, top_count * BLOCK, head_dim
    )
    picked_values = got_values[source, source_rank].reshape(
        row_count, mine_heads, top_count * BLOCK, head_dim
    )
    summed, highest, totals = partial_attention(own_heads, picked_keys, picked_values, score_scale)
    far_summed, far_highest, far_totals = (summed[None], highest[None], totals[None])
    summed, highest, totals = partial_attention(all_heads, recent_keys, recent_values, score_scale)
    near_summed, near_highest, near_totals = (
        lax.all_to_all(summed[None], "group", split_axis=2, concat_axis=0, tiled=True),
        lax.all_to_all(highest[None], "group", split_axis=2, concat_axis=0, tiled=True),
        lax.all_to_all(totals[None], "group", split_axis=2, concat_axis=0, tiled=True),
    )
    merged = combine(
        jnp.concatenate([far_summed, near_summed], axis=0),
        jnp.concatenate([far_highest, near_highest], axis=0),
        jnp.concatenate([far_totals, near_totals], axis=0),
    )
    return merged.reshape(row_count, mine_heads * per_kv * head_dim).astype(jnp.bfloat16)


def solution(mesh):
    return jax.shard_map(
        per_device,
        mesh=mesh,
        in_specs=(
            P("cache", None),
            P("cache"),
            P("cache", "group", None),
            P(None, "group", "cache", None),
            P(None, "group", "cache", None),
            P("cache", None, "group", None),
            P("cache", None, "group", None),
        ),
        out_specs=P("cache", "group"),
        check_vma=False,
    )
```

profile of v0, /device:TPU:0, one launch (start us, length us, event | category | flops | bytes accessed | tf_op | source)
XLA Modules:
  0.0 129.2 jit_solution(7958088049539095475)
XLA Ops:
  0.0 1.0 reshape.470
  1.0 0.7 copy-done
  1.6 0.7 fusion.36
  2.3 0.6 copy.91
  3.0 4.2 %all-to-all-start.1 = ((f32[1,4,8,4]{3,1,0,2:T(4,128)}), f32[1,4,8,4]{3,1,0,2:T(4,128)S(1)}, u32[]{:S(2)}, u32[]{:S(2)}) async-start(f32[1,4,8,4]{3,1,0,2:T(4,128)} %copy.91), calls=%async_computation.1 | async-start | bytes 32768 | tf_op jit(solution)/shard_map/all_to_all | solution.py:114
  7.2 31.5 %all_gather.6 = s32[32,2,4]{2,1,0:T(2,128)S(1)} all-gather(s32[4,2,4]{2,1,0:T(2,128)S(1)} %copy-done.11), channel_id=1, replica_groups=mesh['cache'=8,'group'=4] {'cache'}, dimensions={0}, use_global_device_ids=true | all-gather | bytes 1152 | tf_op jit(solution)/shard_map/all_gather | solution.py:86
  38.7 0.1 reshape.472
  38.8 0.2 reduce_window_sum.11
  39.0 0.2 select_reduce_fusion
  39.2 0.1 copy.87
  39.3 0.6 dynamic-slice
  40.6 0.2 dynamic-update-slice
  40.8 10.8 %all-reduce = s32[32]{0:T(128)S(1)} all-reduce(s32[32]{0:T(128)S(1)} %dynamic-update-slice), channel_id=1, replica_groups=mesh['cache'=8,'group'=4] {'cache'}, use_global_device_ids=true, to_apply=%add | all-reduce | flops 32 | bytes 256
  51.6 0.2 fusion
  51.8 0.1 reshape.503
  51.9 0.1 reshape.473
  52.0 0.7 gather_fusion.4
  52.6 0.1 gather.19
  52.7 0.1 copy.88
  52.8 0.6 copy.98
  53.4 3.2 %all-to-all-start.4 = ((f32[1,4,8,4]{3,1,0,2:T(4,128)}), f32[1,4,8,4]{3,1,0,2:T(4,128)S(1)}, u32[]{:S(2)}, u32[]{:S(2)}) async-start(f32[1,4,8,4]{3,1,0,2:T(4,128)} %copy.98), calls=%async_computation.4 | async-start | bytes 32768 | tf_op jit(solution)/shard_map/all_to_all | solution.py:115
  56.7 0.1 copy.89
  56.8 0.1 reshape.479
  56.9 1.7 %gather_fusion = bf16[32,128,128]{2,1,0:T(8,128)(2,1)} fusion(bf16[2,2,2,128,128]{4,3,2,1,0:T(8,128)(2,1)S(1)} %bitcast.74, s32[32]{0:T(128)S(1)} %reshape.479), kind=kCustom, calls=%fused_computation | custom fusion | bytes 2097536 | tf_op jit(solution)/shard_map/gather | solution.py:55
  58.6 1.9 %all-to-all-done.4 = f32[1,4,8,4]{3,1,0,2:T(4,128)S(1)} async-done(((f32[1,4,8,4]{3,1,0,2:T(4,128)}), f32[1,4,8,4]{3,1,0,2:T(4,128)S(1)}, u32[]{:S(2)}, u32[]{:S(2)}) %all-to-all-start.4) | async-done | bytes 544 | tf_op jit(solution)/shard_map/all_to_all | solution.py:115
  60.5 0.6 copy-done.9
  61.1 3.6 %all-to-all-start = ((bf16[8,4,128,128]{3,2,1,0:T(8,128)(2,1)}), bf16[8,4,128,128]{3,2,1,0:T(8,128)(2,1)S(1)}, u32[]{:S(2)}, u32[]{:S(2)}) async-start(bf16[8,4,128,128]{3,2,1,0:T(8,128)(2,1)} %bitcast.72), calls=%async_computation | async-start | bytes 2097152 | tf_op jit(solution)/shard_map/all_to_all | solution.py:100
  64.7 1.7 %gather_fusion.2 = bf16[32,128,128]{2,1,0:T(8,128)(2,1)} fusion(bf16[2,2,2,128,128]{4,3,2,1,0:T(8,128)(2,1)S(1)} %bitcast.75, s32[32]{0:T(128)S(1)} %reshape.479), kind=kCustom, calls=%fused_computation.2 | custom fusion | bytes 2097536 | tf_op jit(solution)/shard_map/gather | solution.py:58
  66.4 24.2 %all-to-all-done = bf16[8,4,128,128]{3,2,1,0:T(8,128)(2,1)S(1)} async-done(((bf16[8,4,128,128]{3,2,1,0:T(8,128)(2,1)}), bf16[8,4,128,128]{3,2,1,0:T(8,128)(2,1)S(1)}, u32[]{:S(2)}, u32[]{:S(2)}) %all-to-all-start) | async-done | bytes 1048608 | tf_op jit(solution)/shard_map/all_to_all | solution.py:100
  90.6 1.0 copy-done.1
  91.6 3.6 %all-to-all-start.2 = ((bf16[8,4,128,128]{3,2,1,0:T(8,128)(2,1)}), bf16[8,4,128,128]{3,2,1,0:T(8,128)(2,1)S(1)}, u32[]{:S(2)}, u32[]{:S(2)}) async-start(bf16[8,4,128,128]{3,2,1,0:T(8,128)(2,1)} %bitcast.71), calls=%async_computation.2 | async-start | bytes 2097152 | tf_op jit(solution)/shard_map/all_to_all | solution.py:101
  95.2 0.1 reshape.475
  95.3 0.1 reshape.474
  95.4 2.6 %convolution_bitcast_fusion = f32[1,4,8,4,128]{4,3,2,1,0:T(4,128)S(1)} fusion(bf16[4,8,256,128]{3,2,1,0:T(8,128)(2,1)} %param.13, f32[4,8,4,256]{3,2,1,0:T(4,128)S(1)} %get-tuple-element.12, f32[4,8,4]{2,1,0:T(8,128)S(1)} %copy-done.5), kind=kOutput, calls=%fused_computation.6 | convolution fusion | flops 50364416 | bytes 2294272 | tf_op jit(solution)/shard_map/rhgn,rhnd->rhgd/dot_general | solution.py:17
  98.0 0.6 copy.95
  98.7 0.2 convert_reduce_fusion
  98.9 2.9 %gather_fusion.1 = bf16[32,128,128]{2,1,0:T(8,128)(2,1)} fusion(bf16[8,4,128,128]{3,2,1,0:T(8,128)(2,1)} %copy-done.1, s32[32]{0:T(128)S(1)} %fusion.31), kind=kCustom, calls=%fused_computation.1 | custom fusion | bytes 2097408 | tf_op jit(solution)/shard_map/gather | solution.py:103
  101.8 1.7 %fusion.37 = (f32[4,2,4]{2,1,0:T(2,128)S(1)}, f32[4,2,4,512]{3,2,1,0:T(4,128)S(1)}) fusion(bf16[4,2,512,128]{3,2,1,0:T(8,128)(2,1)} %bitcast.73, bf16[4,8,4,128]{3,2,1,0:T(4,128)(2,1)} %copy-done.6, s32[]{:T(128)S(6)} %select_n.181), kind=kOutput, calls=%fused_computation.93 | convolution fusion | flops 4227040 | bytes 1122436 | tf_op jit(solution)/shard_map/rhgd,rhnd->rhgn/dot_general | solution.py:11
  103.5 0.2 fusion.3
  103.7 0.1 fusion.6
  103.8 17.2 %all-to-all-done.2 = bf16[8,4,128,128]{3,2,1,0:T(8,128)(2,1)S(1)} async-done(((bf16[8,4,128,128]{3,2,1,0:T(8,128)(2,1)}), bf16[8,4,128,128]{3,2,1,0:T(8,128)(2,1)S(1)}, u32[]{:S(2)}, u32[]{:S(2)}) %all-to-all-start.2) | async-done | bytes 1048608 | tf_op jit(solution)/shard_map/all_to_all | solution.py:101
  121.0 3.3 %all-to-all-start.3 = ((f32[1,4,8,4,128]{4,3,1,0,2:T(4,128)}), f32[1,4,8,4,128]{4,3,1,0,2:T(4,128)S(1)}, u32[]{:S(2)}, u32[]{:S(2)}) async-start(f32[1,4,8,4,128]{4,3,1,0,2:T(4,128)} %copy.95), calls=%async_computation.3 | async-start | bytes 131072 | tf_op jit(solution)/shard_map/all_to_all | solution.py:113
  124.2 1.7 %gather_fusion.3 = bf16[32,128,128]{2,1,0:T(8,128)(2,1)} fusion(bf16[8,4,128,128]{3,2,1,0:T(8,128)(2,1)S(1)} %all-to-all-done.2, s32[32]{0:T(128)S(1)} %fusion.31), kind=kCustom, calls=%fused_computation.3 | custom fusion | bytes 2097408 | tf_op jit(solution)/shard_map/gather | solution.py:106
  125.9 1.8 %convolution_bitcast_fusion.1 = f32[1,4,2,4,128]{4,3,2,1,0:T(4,128)S(1)} fusion(bf16[4,2,512,128]{3,2,1,0:T(8,128)(2,1)} %bitcast.76, f32[4,2,4,512]{3,2,1,0:T(4,128)S(1)} %get-tuple-element.14, f32[4,2,4]{2,1,0:T(2,128)S(1)} %get-tuple-element.13), kind=kOutput, calls=%fused_computation.8 | convolution fusion | flops 25182208 | bytes 1130624 | tf_op jit(solution)/shard_map/rhgn,rhnd->rhgd/dot_general | solution.py:17
  127.7 0.6 all-to-all-done.3
  128.3 0.1 fusion.1
  128.4 0.1 divide_convert_fusion
  128.6 0.6 convert_element_type.21
  (41 shorter events, 0.2 us)
Async XLA Ops:
  0.0 1.6 %copy-start = (bf16[4,8,256,128]{3,2,1,0:T(8,128)(2,1)S(1)}, bf16[4,8,256,128]{3,2,1,0:T(8,128)(2,1)}, u32[]{:S(2)}) copy-start(bf16[4,8,256,128]{3,2,1,0:T(8,128)(2,1)} %param.12) | copy-start | bytes 6291460
  0.0 39.3 %copy-start.13 = (u32[32]{0:T(128)S(1)}, u32[32]{0:T(128)}, u32[]{:S(2)}) copy-start(u32[32]{0:T(128)} %constant.190) | copy-start | bytes 388
  0.0 7.2 %copy-start.11 = (s32[4,2,4]{2,1,0:T(2,128)S(1)}, s32[4,2,4]{2,1,0:T(2,128)}, u32[]{:S(2)}) copy-start(s32[4,2,4]{2,1,0:T(2,128)} %param.9) | copy-start | bytes 388
  0.0 40.5 %copy-start.12 = (s32[4]{0:T(128)S(1)}, s32[4]{0:T(128)}, u32[]{:S(2)}) copy-start(s32[4]{0:T(128)} %param.8) | copy-start | bytes 52
  1.6 50.3 %copy-start.6 = (bf16[4,8,4,128]{3,2,1,0:T(4,128)(2,1)}, bf16[4,8,4,128]{3,2,1,0:T(4,128)(2,1)S(1)}, u32[]{:S(2)}) copy-start(bf16[4,8,4,128]{3,2,1,0:T(4,128)(2,1)S(1)} %reshape.470) | copy-start | bytes 98308
  2.3 49.4 %copy-start.4 = (f32[4,8,4]{2,1,0:T(8,128)}, f32[4,8,4]{2,1,0:T(8,128)S(1)}, u32[]{:S(2)}) copy-start(f32[4,8,4]{2,1,0:T(8,128)S(1)} %get-tuple-element.11) | copy-start | bytes 1540
  3.0 50.5 %all-to-all-start.1 = ((f32[1,4,8,4]{3,1,0,2:T(4,128)}), f32[1,4,8,4]{3,1,0,2:T(4,128)S(1)}, u32[]{:S(2)}, u32[]{:S(2)}) async-start(f32[1,4,8,4]{3,1,0,2:T(4,128)} %copy.91), calls=%async_computation.1 | async-start | bytes 32768 | tf_op jit(solution)/shard_map/all_to_all | solution.py:114
  52.0 4.9 %copy-start.2 = (bf16[2,2,256,128]{3,2,1,0:T(8,128)(2,1)S(1)}, bf16[2,2,256,128]{3,2,1,0:T(8,128)(2,1)}, u32[]{:S(2)}) copy-start(bf16[2,2,256,128]{3,2,1,0:T(8,128)(2,1)} %param.10) | copy-start | bytes 786436
  53.4 7.1 %copy-start.7 = (f32[1,4,8,4]{3,1,0,2:T(4,128)}, f32[1,4,8,4]{3,1,0,2:T(4,128)S(1)}, u32[]{:S(2)}) copy-start(f32[1,4,8,4]{3,1,0,2:T(4,128)S(1)} %all-to-all-done.1) | copy-start | bytes 1540
  53.4 7.1 %all-to-all-start.4 = ((f32[1,4,8,4]{3,1,0,2:T(4,128)}), f32[1,4,8,4]{3,1,0,2:T(4,128)S(1)}, u32[]{:S(2)}, u32[]{:S(2)}) async-start(f32[1,4,8,4]{3,1,0,2:T(4,128)} %copy.98), calls=%async_computation.4 | async-start | bytes 32768 | tf_op jit(solution)/shard_map/all_to_all | solution.py:115
  56.9 7.8 %copy-start.3 = (bf16[2,2,256,128]{3,2,1,0:T(8,128)(2,1)S(1)}, bf16[2,2,256,128]{3,2,1,0:T(8,128)(2,1)}, u32[]{:S(2)}) copy-start(bf16[2,2,256,128]{3,2,1,0:T(8,128)(2,1)} %param.11) | copy-start | bytes 786436
  60.5 0.6 copy-start.9
  61.1 29.5 %all-to-all-start = ((bf16[8,4,128,128]{3,2,1,0:T(8,128)(2,1)}), bf16[8,4,128,128]{3,2,1,0:T(8,128)(2,1)S(1)}, u32[]{:S(2)}, u32[]{:S(2)}) async-start(bf16[8,4,128,128]{3,2,1,0:T(8,128)(2,1)} %bitcast.72), calls=%async_computation | async-start | bytes 2097152 | tf_op jit(solution)/shard_map/all_to_all | solution.py:100
  66.4 29.0 %copy-start.5 = (f32[4,8,4]{2,1,0:T(8,128)S(1)}, f32[4,8,4]{2,1,0:T(8,128)}, u32[]{:S(2)}) copy-start(f32[4,8,4]{2,1,0:T(8,128)} %copy-done.4) | copy-start | bytes 1540
  90.6 1.0 copy-start.1
  90.6 8.3 %copy-start.8 = (f32[1,4,8,4]{3,1,0,2:T(4,128)S(1)}, f32[1,4,8,4]{3,1,0,2:T(4,128)}, u32[]{:S(2)}) copy-start(f32[1,4,8,4]{3,1,0,2:T(4,128)} %copy-done.7) | copy-start | bytes 1540
  90.6 8.3 %copy-start.10 = (f32[1,4,8,4]{3,1,0,2:T(4,128)S(1)}, f32[1,4,8,4]{3,1,0,2:T(4,128)}, u32[]{:S(2)}) copy-start(f32[1,4,8,4]{3,1,0,2:T(4,128)} %copy-done.9) | copy-start | bytes 1540
  91.6 29.3 %all-to-all-start.2 = ((bf16[8,4,128,128]{3,2,1,0:T(8,128)(2,1)}), bf16[8,4,128,128]{3,2,1,0:T(8,128)(2,1)S(1)}, u32[]{:S(2)}, u32[]{:S(2)}) async-start(bf16[8,4,128,128]{3,2,1,0:T(8,128)(2,1)} %bitcast.71), calls=%async_computation.2 | async-start | bytes 2097152 | tf_op jit(solution)/shard_map/all_to_all | solution.py:101
  121.0 7.4 %all-to-all-start.3 = ((f32[1,4,8,4,128]{4,3,1,0,2:T(4,128)}), f32[1,4,8,4,128]{4,3,1,0,2:T(4,128)S(1)}, u32[]{:S(2)}, u32[]{:S(2)}) async-start(f32[1,4,8,4,128]{4,3,1,0,2:T(4,128)} %copy.95), calls=%async_computation.3 | async-start | bytes 131072 | tf_op jit(solution)/shard_map/all_to_all | solution.py:113
where the time goes:
time: 130 us; the launch traced here: 129 us
  waiting for transfers between devices  43.9 us (34%)
  blocking collectives  42.2 us (32%)
  starting transfers between devices  18 us (14%)
  local copies, waits for them, and re-layouts  16.1 us (12%)
  matrix products  6.8 us (5%)
  other arithmetic  1.34 us (1%)
    all_gather x1, blocking collectives, per_device(): lax.all_gather(selected, 'cache', axis=0, tiled=True)  31.5 us
    all_to_all x1, waiting for transfers between devices, per_device(): lax.all_to_all(key_blocks, 'cache', split_axis=0, concat_axis=0, tiled=True)  24.2 us
    all_to_all x1, waiting for transfers between devices, per_device(): lax.all_to_all(value_blocks, 'cache', split_axis=0, concat_axis=0, tiled=...  17.2 us
    unnamed x1, blocking collectives  10.8 us
    dot_general x2, matrix products, partial_attention(): jnp.einsum('rhgn,rhnd->rhgd', exponent, value_rows.astype(jnp.float32), p...  4.38 us
    all_to_all x1, starting transfers between devices, per_device(): lax.all_to_all(highest[None], 'group', split_axis=2, concat_axis=0, tiled...  4.24 us
    all_to_all x1, starting transfers between devices, per_device(): lax.all_to_all(value_blocks, 'cache', split_axis=0, concat_axis=0, tiled=...  3.63 us
    all_to_all x1, starting transfers between devices, per_device(): lax.all_to_all(key_blocks, 'cache', split_axis=0, concat_axis=0, tiled=True)  3.56 us
  transfers between devices with their start and end apart: 5, of which 4 were waited for; matrix products, arithmetic and copies ran while one was open for 15% of the time, Pallas kernels for 0%

commit v1 on v0

v1 whole, which is shorter than its diff:
```python
import jax
import jax.numpy as jnp
from jax import lax
from jax.sharding import PartitionSpec as P

BLOCK = 128
LOW = -1e30
DENSE_LIMIT = 1 << 20


def weighted(exponent, value_rows, spec):
    high = lax.reduce_precision(exponent, 8, 7)
    rest = (exponent - high).astype(jnp.bfloat16)
    both = jnp.stack([high.astype(jnp.bfloat16), rest])
    out = jnp.einsum(spec, both, value_rows, preferred_element_type=jnp.float32)
    return out[0] + out[1]


def pack(summed, highest, totals):
    lead = summed.shape[0]
    rows = summed.shape[1]
    lanes = summed.shape[2]
    extra = jnp.concatenate([highest, totals], axis=1)
    want = -(-2 * rows // lanes) * lanes
    extra = jnp.pad(extra, ((0, 0), (0, want - 2 * rows))).reshape(lead, want // lanes, lanes)
    return jnp.concatenate([summed, extra], axis=1)


def unpack(packed, rows):
    lead = packed.shape[0]
    extra = packed[:, rows:].reshape(lead, -1)
    return packed[:, :rows], extra[:, :rows], extra[:, rows : 2 * rows]


def per_device(queries, request_of, selected, cache_keys, cache_values, recent_keys, recent_values):
    row_count = queries.shape[0]
    heads_kv = recent_keys.shape[1]
    head_dim = recent_keys.shape[3]
    per_kv = queries.shape[1] // (heads_kv * head_dim)
    mine_heads = selected.shape[1]
    top_count = selected.shape[2]
    score_scale = head_dim ** (-0.5)
    owner_count = lax.axis_size("cache")
    group_count = lax.axis_size("group")
    prompt_count = cache_keys.shape[0]
    held = cache_keys.shape[2]
    per_owner = held // BLOCK
    rows = row_count * mine_heads * per_kv

    all_heads = queries.reshape(row_count, heads_kv, per_kv, head_dim)
    own_heads = lax.dynamic_slice_in_dim(
        all_heads, lax.axis_index("group") * mine_heads, mine_heads, 1
    )
    ids = jnp.concatenate(
        [selected, jnp.broadcast_to(request_of[:, None, None], (row_count, mine_heads, 1))], axis=2
    ).astype(jnp.bfloat16)
    ids = jnp.pad(ids, ((0, 0), (0, 0), (0, head_dim - top_count - 1)))
    ask = jnp.concatenate([own_heads, ids[:, :, None, :]], axis=2)
    ask = jnp.broadcast_to(ask[None], (owner_count,) + ask.shape)
    asked = lax.all_to_all(ask, "cache", split_axis=0, concat_axis=0, tiled=True)

    near_scores = (
        jnp.einsum("rhgd,rhnd->rhgn", all_heads, recent_keys, preferred_element_type=jnp.float32)
        * score_scale
    )
    near_highest = jnp.max(near_scores, axis=-1)
    near_exp = jnp.exp(near_scores - near_highest[..., None])
    near_totals = jnp.sum(near_exp, axis=-1)
    near_summed = weighted(near_exp, recent_values, "xrhgn,rhnd->xrhgd")

    def to_groups(array):
        array = array.reshape((row_count, group_count, mine_heads) + array.shape[2:])
        return jnp.moveaxis(array, 1, 0)

    near = pack(
        to_groups(near_summed).reshape(group_count, rows, head_dim),
        to_groups(near_highest).reshape(group_count, rows),
        to_groups(near_totals).reshape(group_count, rows),
    )
    near = lax.all_to_all(near, "group", split_axis=0, concat_axis=0, tiled=True)

    block = jnp.arange(per_owner, dtype=jnp.int32) + lax.axis_index("cache") * per_owner

    def far_attention(asked):
        far_heads = asked[:, :, :, :per_kv]
        far_ids = asked[:, :, :, per_kv, : top_count + 1].astype(jnp.int32)
        wants = jnp.any(far_ids[..., :top_count, None] == block, axis=3)
        prompt = far_ids[..., top_count, None] == jnp.arange(prompt_count, dtype=jnp.int32)
        wants = prompt[..., :, None] & wants[..., None, :]
        wants = jnp.broadcast_to(
            wants[:, :, :, None, :, :, None],
            wants.shape[:3] + (per_kv,) + wants.shape[3:] + (BLOCK,),
        ).reshape(wants.shape[:3] + (per_kv, prompt_count, held))
        scores = (
            jnp.einsum(
                "crhgd,phnd->crhgpn", far_heads, cache_keys, preferred_element_type=jnp.float32
            )
            * score_scale
        )
        scores = jnp.where(wants, scores, LOW)
        highest = jnp.max(scores, axis=(4, 5))
        exponent = jnp.where(wants, jnp.exp(scores - highest[..., None, None]), 0.0)
        totals = jnp.sum(exponent, axis=(4, 5))
        return weighted(exponent, cache_values, "xcrhgpn,phnd->xcrhgd"), highest, totals

    if owner_count * rows * prompt_count * held <= DENSE_LIMIT:
        far_summed, far_highest, far_totals = far_attention(asked)
    else:
        far_summed, far_highest, far_totals = lax.map(lambda one: far_attention(one[None]), asked)
    far = pack(
        far_summed.reshape(owner_count, rows, head_dim),
        far_highest.reshape(owner_count, rows),
        far_totals.reshape(owner_count, rows),
    )
    far = lax.all_to_all(far, "cache", split_axis=0, concat_axis=0, tiled=True)

    parts = jnp.concatenate([near, far], axis=0)
    summed, highest, totals = unpack(parts, rows)
    factor = jnp.exp(highest - jnp.max(highest, axis=0)[None])
    weight = jnp.sum(factor * totals, axis=0)
    merged = jnp.sum(factor[..., None] * summed, axis=0) / weight[..., None]
    return merged.reshape(row_count, mine_heads * per_kv * head_dim).astype(jnp.bfloat16)


def solution(mesh):
    return jax.shard_map(
        per_device,
        mesh=mesh,
        in_specs=(
            P("cache", None),
            P("cache"),
            P("cache", "group", None),
            P(None, "group", "cache", None),
            P(None, "group", "cache", None),
            P("cache", None, "group", None),
            P("cache", None, "group", None),
        ),
        out_specs=P("cache", "group"),
        check_vma=False,
    )
```

time: 130 us -> 37.4 us (0.29)
  blocking collectives: 42.2 us -> 0 us
  waiting for transfers between devices: 43.9 us -> 13.1 us
  local copies, waits for them, and re-layouts: 16.1 us -> 4.01 us
  matrix products: 6.8 us -> 1.78 us
  starting transfers between devices: 18 us -> 14 us
  other arithmetic: 1.34 us -> 3.84 us
    all_gather x1 -> x0, blocking collectives: 31.5 us -> none  [per_device(): lax.all_gather(selected, 'cache', axis=0, tiled=True)]
    all_to_all x5 -> x3, waiting for transfers between devices: 43.9 us -> 13.1 us  [the longest x1 7.49 us: per_device(): far = lax.all_to_all(far, 'cache', split_axis=0, concat_axis=0, tiled=True)]
    unnamed x1 -> x0, blocking collectives: 10.8 us -> none
    gather x9 -> x0, local copies, waits for them, and re-layouts: 8.98 us -> none  [the longest x1 2.89 us: per_device(): got_keys[source, source_rank]]
    dot_general x4, matrix products: 6.8 us -> 1.78 us  [the longest x2 0.73 us: weighted(): out = jnp.einsum(spec, both, value_rows, preferred_element_type=jnp.float32)]
    all_to_all x5 -> x3, starting transfers between devices: 18 us -> 14 us  [the longest x1 7.31 us: per_device(): lax.all_to_all(ask, 'cache', split_axis=0, concat_axis=0, tiled=True)]
    unnamed x31 -> x11, local copies, waits for them, and re-layouts: 3.15 us -> 0.71 us
    another operation x1 -> x4, other arithmetic: 0.18 us -> 1.89 us  [owner_plan(): rank_here = jnp.cumsum(held_here.astype(jnp.int32), axis=1) - 1]
  transfers between devices with their start and end apart: 5 -> 3, of which waited for: 4 -> 3; matrix products, arithmetic and copies ran while one was open for 15% -> 13% of each run, Pallas kernels for 0% -> 0%
where the time goes in v1:
time: 37.4 us; the launch traced here: 36.9 us
  starting transfers between devices  14 us (37%)
  waiting for transfers between devices  13.1 us (35%)
  local copies, waits for them, and re-layouts  4.01 us (11%)
  other arithmetic  3.84 us (10%)
  matrix products  1.78 us (5%)
    all_to_all x1, waiting for transfers between devices, per_device(): far = lax.all_to_all(far, 'cache', split_axis=0, concat_axis=0, tiled=True)  7.49 us
    all_to_all x1, starting transfers between devices, per_device(): lax.all_to_all(ask, 'cache', split_axis=0, concat_axis=0, tiled=True)  7.31 us
    all_to_all x1, waiting for transfers between devices, per_device(): lax.all_to_all(ask, 'cache', split_axis=0, concat_axis=0, tiled=True)  4.01 us
    all_to_all x1, starting transfers between devices, per_device(): far = lax.all_to_all(far, 'cache', split_axis=0, concat_axis=0, tiled=True)  3.38 us
    all_to_all x1, starting transfers between devices, per_device(): lax.all_to_all(near, 'group', split_axis=0, concat_axis=0, tiled=True)  3.29 us
    all_to_all x1, waiting for transfers between devices, per_device(): lax.all_to_all(near, 'group', split_axis=0, concat_axis=0, tiled=True)  1.59 us
    another operation x2, other arithmetic  1.35 us
    reshape x1, local copies, waits for them, and re-layouts, per_device(): all_heads = queries.reshape(row_count, heads_kv, per_kv, head_dim)  0.95 us
  transfers between devices with their start and end apart: 3, of which 3 were waited for; matrix products, arithmetic and copies ran while one was open for 13% of the time, Pallas kernels for 0%

profile of v1, /device:TPU:0, one launch (start us, length us, event | category | flops | bytes accessed | tf_op | source)
XLA Modules:
  0.0 36.9 jit_solution(14548966600770726459)
XLA Ops:
  0.0 0.0 copy-start
  0.0 1.0 %reshape.69 = bf16[4,8,4,128]{3,2,1,0:T(4,128)(2,1)S(1)} reshape(bf16[4,4096]{1,0:T(4,128)(2,1)} %param.7) | data formatting | bytes 65536 | tf_op jit(solution)/shard_map/reshape | solution.py:50
  1.0 0.7 %convert.9 = bf16[4]{0:T(256)(128)(2,1)S(1)} convert(s32[4]{0:T(128)} %param.8) | non-fusion elementwise | flops 4 | bytes 24 | tf_op jit(solution)/shard_map/convert.3
  1.6 0.7 %convert.8 = bf16[4,2,4]{2,1,0:T(2,128)(2,1)S(1)} convert(s32[4,2,4]{2,1,0:T(2,128)} %param.9) | non-fusion elementwise | flops 32 | bytes 192 | tf_op jit(solution)/shard_map/convert.1
  2.3 0.1 broadcast_in_dim.18
  2.4 0.1 fusion.27
  2.5 0.6 %broadcast_in_dim.21 = bf16[8,4,2,5,128]{4,1,3,2,0:T(4,128)(2,1)} broadcast(bf16[4,2,5,128]{3,0,2,1:T(4,128)(2,1)S(1)} %copy.75), dimensions={1,2,3,4} | broadcast | bytes 92160 | tf_op jit(solution)/shard_map/broadcast_in_dim | solution.py:59
  3.2 7.3 %all-to-all-start.1 = ((bf16[8,4,2,5,128]{4,1,3,2,0:T(4,128)(2,1)}), bf16[8,4,2,5,128]{4,1,3,2,0:T(4,128)(2,1)S(1)}, u32[]{:S(2)}, u32[]{:S(2)}) async-start(bf16[8,4,2,5,128]{4,1,3,2,0:T(4,128)(2,1)} %broadcast_in_dim.21), calls=%async_computation.1 | async-start | bytes 163840 | tf_op jit(solution)/shard_map/all_to_all | solution.py:60
  10.5 0.0 copy-done
  10.5 0.0 copy-start.1
  10.5 0.7 %fusion.28 = (f32[4,8,4]{2,1,0:T(8,128)S(1)}, f32[4,8,4,256]{3,2,1,0:T(4,128)S(1)}) fusion(bf16[4,8,4,128]{3,2,1,0:T(4,128)(2,1)S(1)} %reshape.69, bf16[4,8,256,128]{3,2,1,0:T(8,128)(2,1)S(1)} %copy-done), kind=kOutput, calls=%fused_computation.64 | convolution fusion | flops 8454016 | bytes 2261504 | tf_op jit(solution)/shard_map/rhgd,rhnd->rhgn/dot_general | solution.py:63
  11.2 0.0 copy-start.2
  11.2 0.2 fusion.19
  11.5 0.6 %copy-done.1 = bf16[4,8,256,128]{3,2,1,0:T(8,128)(2,1)S(1)} copy-done((bf16[4,8,256,128]{3,2,1,0:T(8,128)(2,1)S(1)}, bf16[4,8,256,128]{3,2,1,0:T(8,128)(2,1)}, u32[]{:S(2)}) %copy-start.1) | copy-done | bytes 2097176
  12.1 0.4 %fusion.4 = f32[2,4,8,4,128]{4,3,0,2,1:T(4,128)S(1)} fusion(bf16[4,8,256,128]{3,2,1,0:T(8,128)(2,1)S(1)} %copy-done.1, bf16[1,4,8,4,256]{4,3,2,1,0:T(4,128)(2,1)S(1)} %get-tuple-element.11, bf16[1,4,8,4,256]{4,3,2,1,0:T(4,128)(2,1)S(1)} %get-tuple-element.10), kind=kOutput, calls=%fused_computation.6 | convolution fusion | flops 16842752 | bytes 2359296 | tf_op jit(solution)/shard_map/xrhgn,rhnd->xrhgd/dot_general | solution.py:15
  12.5 0.0 copy-start.3
  12.6 0.1 reshape.74
  12.7 0.1 reshape.72
  12.8 0.1 select_maximum_fusion.1
  12.9 0.6 %pad_maximum_fusion.3 = f32[4,33,128]{2,1,0:T(8,128)} fusion(f32[4,1,128]{2,1,0:T(1,128)S(1)} %bitcast.90, f32[4,32,128]{2,1,0:T(8,128)S(1)} %bitcast.82), kind=kLoop, calls=%fused_computation.29 | loop fusion | flops 16896 | bytes 135168 | tf_op jit(solution)/shard_map/concatenate | solution.py:26
  13.5 4.0 %all-to-all-done.1 = bf16[8,4,2,5,128]{4,1,3,2,0:T(4,128)(2,1)S(1)} async-done(((bf16[8,4,2,5,128]{4,1,3,2,0:T(4,128)(2,1)}), bf16[8,4,2,5,128]{4,1,3,2,0:T(4,128)(2,1)S(1)}, u32[]{:S(2)}, u32[]{:S(2)}) %all-to-all-start.1) | async-done | bytes 81952 | tf_op jit(solution)/shard_map/all_to_all | solution.py:60
  17.5 3.3 %all-to-all-start = ((f32[4,33,128]{2,1,0:T(8,128)}), f32[4,33,128]{2,1,0:T(8,128)S(1)}, u32[]{:S(2)}, u32[]{:S(2)}) async-start(f32[4,33,128]{2,1,0:T(8,128)} %pad_maximum_fusion.3), calls=%async_computation | async-start | bytes 163840 | tf_op jit(solution)/shard_map/all_to_all | solution.py:80
  20.8 0.1 slice.51
  20.9 0.1 copy.77
  21.0 0.1 copy.76
  21.2 0.1 compare_reduce_fusion
  21.3 0.1 broadcast_bitcast_fusion
  21.5 0.0 copy-done.2
  21.5 0.3 fusion.29
  21.8 0.3 fusion.11
  22.1 0.0 copy-done.3
  22.1 0.3 convolution_bitcast_fusion
  22.5 0.1 copy.87
  22.5 0.1 copy.86
  22.6 0.1 fusion.23
  22.7 0.7 %copy.88 = f32[8,33,128]{2,1,0:T(8,128)} copy(f32[8,33,128]{2,0,1:T(8,128)S(1)} %pad_maximum_fusion.1) | data formatting | bytes 270336 | tf_op jit(solution)/shard_map/concatenate | solution.py:26
  23.4 1.6 %all-to-all-done = f32[4,33,128]{2,1,0:T(8,128)S(1)} async-done(((f32[4,33,128]{2,1,0:T(8,128)}), f32[4,33,128]{2,1,0:T(8,128)S(1)}, u32[]{:S(2)}, u32[]{:S(2)}) %all-to-all-start) | async-done | bytes 67616 | tf_op jit(solution)/shard_map/all_to_all | solution.py:80
  25.0 3.4 %all-to-all-start.2 = ((f32[8,33,128]{2,1,0:T(8,128)}), f32[8,33,128]{2,1,0:T(8,128)S(1)}, u32[]{:S(2)}, u32[]{:S(2)}) async-start(f32[8,33,128]{2,1,0:T(8,128)} %copy.88), calls=%async_computation.2 | async-start | bytes 327680 | tf_op jit(solution)/shard_map/all_to_all | solution.py:115
  28.4 7.5 %all-to-all-done.2 = f32[8,33,128]{2,1,0:T(8,128)S(1)} async-done(((f32[8,33,128]{2,1,0:T(8,128)}), f32[8,33,128]{2,1,0:T(8,128)S(1)}, u32[]{:S(2)}, u32[]{:S(2)}) %all-to-all-start.2) | async-done | bytes 135200 | tf_op jit(solution)/shard_map/all_to_all | solution.py:115
  35.9 0.1 fusion.22
  36.0 0.1 fusion.14
  36.2 0.1 div.13
  36.2 0.1 broadcast_bitcast_fusion.1
  36.3 0.6 %fusion.21 = bf16[4,1024]{1,0:T(4,128)(2,1)} fusion(f32[4,1024]{1,0:T(4,128)S(1)} %reduce_sum.41, f32[1,4,8,128]{3,2,1,0:T(8,128)S(1)} %broadcast_bitcast_fusion.1), kind=kLoop, calls=%fused_computation.41 | loop fusion | flops 8192 | bytes 40960 | tf_op jit(solution)/shard_map/convert_element_type | solution.py:122
  (24 shorter events, 0.3 us)
Async XLA Ops:
  0.0 10.5 %copy-start = (bf16[4,8,256,128]{3,2,1,0:T(8,128)(2,1)S(1)}, bf16[4,8,256,128]{3,2,1,0:T(8,128)(2,1)}, u32[]{:S(2)}) copy-start(bf16[4,8,256,128]{3,2,1,0:T(8,128)(2,1)} %param.12) | copy-start | bytes 6291460
  3.2 14.3 %all-to-all-start.1 = ((bf16[8,4,2,5,128]{4,1,3,2,0:T(4,128)(2,1)}), bf16[8,4,2,5,128]{4,1,3,2,0:T(4,128)(2,1)S(1)}, u32[]{:S(2)}, u32[]{:S(2)}) async-start(bf16[8,4,2,5,128]{4,1,3,2,0:T(4,128)(2,1)} %broadcast_in_dim.21), calls=%async_computation.1 | async-start | bytes 163840 | tf_op jit(solution)/shard_map/all_to_all | solution.py:60
  10.5 1.6 %copy-start.1 = (bf16[4,8,256,128]{3,2,1,0:T(8,128)(2,1)S(1)}, bf16[4,8,256,128]{3,2,1,0:T(8,128)(2,1)}, u32[]{:S(2)}) copy-start(bf16[4,8,256,128]{3,2,1,0:T(8,128)(2,1)} %param.13) | copy-start | bytes 6291460
  11.2 10.2 %copy-start.2 = (bf16[2,2,256,128]{3,2,1,0:T(8,128)(2,1)S(1)}, bf16[2,2,256,128]{3,2,1,0:T(8,128)(2,1)}, u32[]{:S(2)}) copy-start(bf16[2,2,256,128]{3,2,1,0:T(8,128)(2,1)} %param.10) | copy-start | bytes 786436
  12.5 9.6 %copy-start.3 = (bf16[2,2,256,128]{3,2,1,0:T(8,128)(2,1)S(1)}, bf16[2,2,256,128]{3,2,1,0:T(8,128)(2,1)}, u32[]{:S(2)}) copy-start(bf16[2,2,256,128]{3,2,1,0:T(8,128)(2,1)} %param.11) | copy-start | bytes 786436
  17.5 7.5 %all-to-all-start = ((f32[4,33,128]{2,1,0:T(8,128)}), f32[4,33,128]{2,1,0:T(8,128)S(1)}, u32[]{:S(2)}, u32[]{:S(2)}) async-start(f32[4,33,128]{2,1,0:T(8,128)} %pad_maximum_fusion.3), calls=%async_computation | async-start | bytes 163840 | tf_op jit(solution)/shard_map/all_to_all | solution.py:80
  25.0 10.9 %all-to-all-start.2 = ((f32[8,33,128]{2,1,0:T(8,128)}), f32[8,33,128]{2,1,0:T(8,128)S(1)}, u32[]{:S(2)}, u32[]{:S(2)}) async-start(f32[8,33,128]{2,1,0:T(8,128)} %copy.88), calls=%async_computation.2 | async-start | bytes 327680 | tf_op jit(solution)/shard_map/all_to_all | solution.py:115
